TPU v7x, 32 devices: a whole 2x2x4 slice. The times are simulated.
32 devices in a mesh: ctx: 8 (over y, x, core), fsdp: 4 (over z).
Axes of the slice: x: 2, y: 2, z: 4, core: 2. Of those that a mesh axis runs over, the one named last changes fastest.
Arguments:
- inputs: bfloat16 [4, 1024, 1536], P('fsdp', 'ctx')
- positions: int32 [4, 1024], P('fsdp', 'ctx'), may hold values from 0 to 1535, as said below
- block_order: int32 [16], replicated, may hold values from 0 to 15, as said below
- attention_gain: bfloat16 [1536], P('fsdp'), may hold values from 0.5 to 1.5
- projection: bfloat16 [1536, 2048], P('fsdp')
- projection_bias: bfloat16 [2048], P('fsdp'), may hold values from -4 to 4
- output_weight: bfloat16 [1536, 1536], P('fsdp'), may hold values from -1.5 to 1.5
- feedforward_gain: bfloat16 [1536], P('fsdp'), may hold values from 0.5 to 1.5
- gate_up: bfloat16 [1536, 17920], P('fsdp'), may hold values from -0.15625 to 0.15625
- down_weight: bfloat16 [8960, 1536], P('fsdp'), may hold values from -0.0625 to 0.0625
- cotangent: bfloat16 [4, 1024, 1536], P('fsdp', 'ctx'), may hold values from -6 to 6
Outputs:
- outputs: bfloat16 [4, 1024, 1536], P('fsdp', 'ctx')
- gradient: bfloat16 [4, 1024, 1536], P('fsdp', 'ctx')
- gradient_attention_gain: float32 [1536], P(('ctx', 'fsdp'))
- gradient_projection: float32 [1536, 2048], P('fsdp', 'ctx')
- gradient_projection_bias: float32 [2048], P(('ctx', 'fsdp'))
- gradient_output: float32 [1536, 1536], P('fsdp', 'ctx')
- gradient_feedforward_gain: float32 [1536], P(('ctx', 'fsdp'))
- gradient_gate_up: float32 [1536, 17920], P('fsdp', 'ctx')
- gradient_down: float32 [8960, 1536], P('fsdp', 'ctx')
Inputs may be any that keep to these rules, and one draw needn't show every extreme that they name: `block_order`: A permutation: each of 0 to 15 appears once. Within each sequence, positions grow strictly with order_index; the sequence's first token has position 0, and of the 1023 steps between tokens next to each other in the sequence exactly 512 are 2 and the others are 1, so the last token has position 1535.
All inputs are finite; a program needn't handle non-finite values.
Results may differ from a plain program's by a relative error of at most 0.02.
Values may be sent and summed in bfloat16 or wider, within the bound.
A program may use at most 320 MiB of HBM per device.

v0:
```python
import math
import jax
import jax.numpy as jnp
from jax import lax
from jax.sharding import PartitionSpec as P

HEADS = 12
KV_HEADS = 2
HEAD = 128
FF = 8960
GROUP = 2
EPS = 1e-06
THETA = 1000000.0
NEGATIVE = -1e30
BF = jnp.bfloat16
F32 = jnp.float32


def rope_tables(places):
    freq = THETA ** (-jnp.arange(0, HEAD, 2).astype(F32) / HEAD)
    angle = places.astype(F32)[:, None] * freq[None, :]
    angle = jnp.concatenate([angle, angle], axis=-1)
    return (jnp.cos(angle), jnp.sin(angle))


def rotate(values):
    middle = values.shape[-1] // 2
    return jnp.concatenate([-values[..., middle:], values[..., :middle]], axis=-1)


def apply_rope(values, cosine, sine):
    return values * cosine[:, None, :] + rotate(values) * sine[:, None, :]


def rope_back(grads, cosine, sine):
    return grads * cosine[:, None, :] - rotate(grads * sine[:, None, :])


def order_rows(block_order, start, count, half):
    offsets = start + jnp.arange(count, dtype=jnp.int32)
    slots = offsets // half
    table = jnp.arange(block_order.shape[0], dtype=jnp.int32)
    picked = jnp.sum(jnp.where(slots[:, None] == table[None, :], block_order[None, :], 0), axis=1)
    return picked * half + offsets % half


def rms_inverse(values):
    return lax.rsqrt(jnp.mean(values * values, axis=-1, keepdims=True) + EPS)


def norm_back(d_normed, values, inverse, gain):
    unit = values * inverse
    d_unit = d_normed * gain
    d_gain = jnp.sum(d_normed * unit, axis=0)
    d_values = inverse * (d_unit - unit * jnp.mean(d_unit * unit, axis=-1, keepdims=True))
    return (d_values, d_gain)


def dot(left, right, dims, out=F32):
    return lax.dot_general(left, right, (dims, ((), ())), preferred_element_type=out)


def swapped(x, size):
    return lax.ppermute(x, "fsdp", [(i, i ^ 1) for i in range(size)])


def gather_tokens(x, size):
    both = jnp.stack([x, swapped(x, size)])
    return lax.all_gather(both, "ctx", axis=1, tiled=True)


def scatter_tokens(partial, size):
    parts = lax.psum_scatter(partial, "ctx", scatter_dimension=1, tiled=True)
    return parts[0].astype(F32) + swapped(parts[1], size).astype(F32)


def body(
    inputs,
    positions,
    block_order,
    attention_gain,
    projection,
    projection_bias,
    output_weight,
    feedforward_gain,
    gate_up,
    down_weight,
    cotangent,
):
    rows, width = inputs.shape[1:]
    half = rows // 2
    ratio = HEADS // KV_HEADS
    query_width = HEADS * HEAD
    key_width = KV_HEADS * HEAD
    cycle = lax.axis_size("ctx")
    owners = lax.axis_size("fsdp")
    place = lax.axis_index("ctx")
    owner = lax.axis_index("fsdp")
    fold = owners // GROUP
    unit = FF // (owners * cycle)
    depth = width // owners
    length = rows * cycle
    slab = depth // cycle
    whole_projection = lax.all_gather(
        lax.dynamic_slice_in_dim(projection, place * slab, slab, 0),
        ("fsdp", "ctx"),
        axis=0,
        tiled=True,
    )
    whole_output = lax.all_gather(
        lax.dynamic_slice_in_dim(output_weight, place * slab, slab, 0),
        ("fsdp", "ctx"),
        axis=0,
        tiled=True,
    )
    small = lax.all_gather(
        jnp.concatenate([attention_gain, feedforward_gain, projection_bias]), "fsdp", axis=0
    )
    gain_one = small[:, :depth].reshape(-1).astype(F32)
    gain_two = small[:, depth : 2 * depth].reshape(-1).astype(F32)
    bias = small[:, 2 * depth :].reshape(-1).astype(F32)
    pieces = []
    for side in range(2):
        for plane in range(owners):
            start = side * FF + plane * (FF // owners) + place * unit
            pieces.append(lax.dynamic_slice_in_dim(gate_up, start, unit, 1))

    def part(side, to):
        return jnp.concatenate(
            [pieces[side * owners + (to + GROUP * b) % owners] for b in range(fold)], axis=1
        )

    sent = jnp.stack([jnp.stack([part(side, to) for side in range(2)]) for to in range(owners)])
    got = lax.all_to_all(sent, "fsdp", split_axis=0, concat_axis=0, tiled=True)
    gate_weight = got[:, 0].reshape(width, fold * unit)
    up_weight = got[:, 1].reshape(width, fold * unit)
    own_down = lax.dynamic_slice_in_dim(down_weight, place * unit, unit, 0)
    down = [own_down]
    for b in range(1, fold):
        route = [((i + GROUP * b) % owners, i) for i in range(owners)]
        down.append(lax.ppermute(own_down, "fsdp", route))
    down = jnp.concatenate(down, axis=0)
    tangent = cotangent[0]
    tangents = gather_tokens(tangent, owners).reshape(GROUP * length, width)
    features = inputs[0].astype(F32)
    inverse_one = rms_inverse(features)
    normed_one = (features * inverse_one * gain_one).astype(BF)
    projected = dot(normed_one, whole_projection, ((1,), (0,))) + bias
    cosine, sine = rope_tables(positions[0])
    queries = apply_rope(
        projected[:, :query_width].reshape(rows, HEADS, HEAD), cosine, sine
    ).astype(BF)
    keys = apply_rope(
        projected[:, query_width : query_width + key_width].reshape(rows, KV_HEADS, HEAD),
        cosine,
        sine,
    ).astype(BF)
    values = projected[:, query_width + key_width :].astype(BF)
    pairs = lax.all_gather(
        jnp.concatenate([keys.reshape(rows, key_width), values], axis=1), "ctx", axis=0, tiled=True
    )
    all_keys = pairs[:, :key_width].reshape(length, KV_HEADS, HEAD)
    all_values = pairs[:, key_width:].reshape(length, KV_HEADS, HEAD)
    grouped = queries.reshape(rows, KV_HEADS, ratio, HEAD).transpose(1, 2, 0, 3)
    own_index = order_rows(block_order, place * rows, rows, half)
    all_index = order_rows(block_order, 0, length, half)
    mask = (all_index[None, :] <= own_index[:, None])[None, None]
    scale = 1.0 / math.sqrt(HEAD)

    def weights_of():
        scores = jnp.einsum("grqd,kgd->grqk", grouped, all_keys, preferred_element_type=F32) * scale
        return jnp.where(mask, scores, NEGATIVE)

    scores = weights_of()
    top = jnp.max(scores, axis=-1, keepdims=True)
    probs = jnp.exp(scores - top)
    total = jnp.sum(probs, axis=-1, keepdims=True)
    probs = probs / total
    low_probs = probs.astype(BF)
    attention = jnp.einsum("grqk,kgd->grqd", low_probs, all_values, preferred_element_type=F32)
    merged = attention.transpose(2, 0, 1, 3).reshape(rows, query_width).astype(BF)
    residual = features + dot(merged, whole_output, ((1,), (0,)))
    inverse_two = rms_inverse(residual)
    normed_two = (residual * inverse_two * gain_two).astype(BF)
    tokens = gather_tokens(normed_two, owners).reshape(GROUP * length, width)
    gate = dot(tokens, gate_weight, ((1,), (0,)))
    upward = dot(tokens, up_weight, ((1,), (0,)))
    sigmoid = jax.nn.sigmoid(gate)
    activation = (gate * sigmoid * upward).astype(BF)
    branch = dot(activation, down, ((1,), (0,)), BF).reshape(GROUP, length, width)
    outputs = (residual + scatter_tokens(branch, owners)).astype(BF)
    d_activation = dot(tangents, down, ((1,), (1,)))
    d_gate = (d_activation * upward * sigmoid * (1.0 + gate * (1.0 - sigmoid))).astype(BF)
    d_upward = (d_activation * gate * sigmoid).astype(BF)
    d_tokens = (
        dot(d_gate, gate_weight, ((1,), (1,))) + dot(d_upward, up_weight, ((1,), (1,)))
    ).astype(BF)
    d_normed_two = scatter_tokens(d_tokens.reshape(GROUP, length, width), owners)
    grad_gate = dot(tokens, d_gate, ((0,), (0,)), BF)
    grad_up = dot(tokens, d_upward, ((0,), (0,)), BF)
    grad_down = dot(activation, tangents, ((0,), (0,)), BF)
    mine = lax.all_to_all(
        jnp.stack([grad_gate.reshape(owners, depth, -1), grad_up.reshape(owners, depth, -1)], 1),
        "fsdp",
        split_axis=0,
        concat_axis=0,
        tiled=True,
    )
    folded = []
    for plane in range(owners):
        total_piece = 0.0
        for source in range(plane % GROUP, owners, GROUP):
            b = (plane - source) // GROUP % fold
            total_piece = total_piece + mine[source, :, :, b * unit : (b + 1) * unit].astype(F32)
        folded.append(total_piece.astype(BF))
    folded = jnp.stack(folded, axis=1)
    spread = lax.all_to_all(
        folded.reshape(cycle, 2 * owners // cycle, depth, unit),
        "ctx",
        split_axis=0,
        concat_axis=0,
        tiled=True,
    )
    final_gate_up = spread.transpose(2, 1, 0, 3).reshape(depth, -1).astype(F32)
    grad_down = grad_down.reshape(fold, unit, width)
    total_down = grad_down[0].astype(F32)
    for b in range(1, fold):
        route = [(i, (i + GROUP * b) % owners) for i in range(owners)]
        total_down = total_down + lax.ppermute(grad_down[b], "fsdp", route).astype(F32)
    final_down = (
        lax.all_to_all(
            total_down.astype(BF).reshape(unit, cycle, width // cycle).transpose(1, 0, 2),
            "ctx",
            split_axis=0,
            concat_axis=0,
            tiled=True,
        )
        .reshape(-1, width // cycle)
        .astype(F32)
    )
    d_residual, grad_gain_two = norm_back(d_normed_two, residual, inverse_two, gain_two)
    d_residual = d_residual + tangent.astype(F32)
    d_branch = d_residual.astype(BF)
    d_merged = dot(d_branch, whole_output, ((1,), (1,))).astype(BF)
    d_attention = d_merged.reshape(rows, KV_HEADS, ratio, HEAD).transpose(1, 2, 0, 3)
    delta = jnp.sum(d_attention.astype(F32) * attention, axis=-1, keepdims=True)
    d_values = jnp.einsum("grqk,grqd->kgd", low_probs, d_attention, preferred_element_type=F32)
    d_probs = jnp.einsum("grqd,kgd->grqk", d_attention, all_values, preferred_element_type=F32)
    d_scores = (probs * (d_probs - delta)).astype(BF)
    d_queries = jnp.einsum("grqk,kgd->qgrd", d_scores, all_keys, preferred_element_type=F32) * scale
    d_keys = jnp.einsum("grqk,grqd->kgd", d_scores, grouped, preferred_element_type=F32) * scale
    d_pairs = jnp.concatenate(
        [d_keys.reshape(length, key_width), d_values.reshape(length, key_width)], axis=1
    ).astype(BF)
    d_pairs = lax.psum_scatter(d_pairs, "ctx", scatter_dimension=0, tiled=True).astype(F32)
    d_query_raw = rope_back(d_queries.reshape(rows, HEADS, HEAD), cosine, sine)
    d_key_raw = rope_back(d_pairs[:, :key_width].reshape(rows, KV_HEADS, HEAD), cosine, sine)
    d_projected = jnp.concatenate(
        [
            d_query_raw.reshape(rows, query_width),
            d_key_raw.reshape(rows, key_width),
            d_pairs[:, key_width:],
        ],
        axis=1,
    ).astype(BF)
    grad_bias = jnp.sum(d_projected.astype(F32), axis=0)
    d_normed_one = dot(d_projected, whole_projection, ((1,), (1,)))
    d_features, grad_gain_one = norm_back(d_normed_one, features, inverse_one, gain_one)
    gradient = (d_residual + d_features).astype(BF)

    def columns_home(left, right):
        whole_left = lax.all_gather(left, "ctx", axis=0, tiled=True)
        share = right.shape[1] // cycle
        sliced = lax.all_to_all(
            right.reshape(rows, cycle, share).transpose(1, 0, 2),
            "ctx",
            split_axis=0,
            concat_axis=0,
            tiled=True,
        ).reshape(length, share)
        partial = dot(whole_left, sliced, ((0,), (0,)), BF).reshape(owners, depth, share)
        parts = lax.all_to_all(partial, "fsdp", split_axis=0, concat_axis=0, tiled=True)
        return jnp.sum(parts.astype(F32), axis=0)

    final_output = columns_home(merged, d_branch)
    final_projection = columns_home(normed_one, d_projected)
    count = owners * cycle
    sums = jnp.concatenate(
        [
            grad_gain_one.reshape(count, -1),
            grad_bias.reshape(count, -1),
            grad_gain_two.reshape(count, -1),
        ],
        axis=1,
    )
    sums = lax.psum_scatter(sums, ("ctx", "fsdp"), scatter_dimension=0, tiled=True)[0]
    first = width // count
    last = sums.shape[0] - first
    return (
        outputs[None],
        gradient[None],
        sums[:first],
        final_projection,
        sums[first:last],
        final_output,
        sums[last:],
        final_gate_up,
        final_down,
    )


def solution(mesh):
    return jax.shard_map(
        body,
        mesh=mesh,
        in_specs=(
            P("fsdp", "ctx", None),
            P("fsdp", "ctx"),
            P(),
            P("fsdp"),
            P("fsdp", None),
            P("fsdp"),
            P("fsdp", None),
            P("fsdp"),
            P("fsdp", None),
            P("fsdp", None),
            P("fsdp", "ctx", None),
        ),
        out_specs=(
            P("fsdp", "ctx", None),
            P("fsdp", "ctx", None),
            P(("ctx", "fsdp")),
            P("fsdp", "ctx"),
            P(("ctx", "fsdp")),
            P("fsdp", "ctx"),
            P(("ctx", "fsdp")),
            P("fsdp", "ctx"),
            P("fsdp", "ctx"),
        ),
        check_vma=False,
    )
```

profile of v0, /device:TPU:0, one launch (start us, length us, event | category | flops | bytes accessed | tf_op | source)
XLA Modules:
  0.0 765.0 jit_solution(17226624631359661983)
XLA Ops:
  10.1 14.9 %all-gather.1 = bf16[4,1,1280]{2,1,0:T(2,128)(2,1)S(1)} all-gather(bf16[1,1,1280]{2,1,0:T(2,128)(2,1)S(1)} %reshape.500), channel_id=2, replica_groups=mesh['ctx'=8,'fsdp'=4] {'fsdp'}, dimensions={0}, use_global_device_ids=true | all-gather | bytes 12800 | tf_op jit(solution)/shard_map/all_gather | solution.py:116
  28.6 54.7 %all-gather.10.cloned.1.call-done = bf16[1536,2048]{1,0:T(8,128)(2,1)} async-done(((bf16[48,2048]{1,0:T(8,128)(2,1)}), bf16[1536,2048]{1,0:T(8,128)(2,1)}) %all-gather.10.cloned.1.call-update) | async-done | bytes 6291472 | tf_op jit(solution)/shard_map/all_gather | solution.py:104
  91.2 19.4 %all-gather.12.cloned.1.call-done = bf16[1024,512]{1,0:T(8,128)(2,1)} async-done(((bf16[128,512]{1,0:T(8,128)(2,1)}), bf16[1024,512]{1,0:T(8,128)(2,1)}) %all-gather.12.cloned.1.call-update) | async-done | bytes 1048592 | tf_op jit(solution)/shard_map/all_gather | solution.py:159
  112.5 4.8 fusion.70
  123.7 53.9 %all-gather.14.cloned.1.call-done = bf16[1536,1536]{1,0:T(8,128)(2,1)} async-done(((bf16[48,1536]{1,0:T(8,128)(2,1)}), bf16[1536,1536]{1,0:T(8,128)(2,1)}) %all-gather.14.cloned.1.call-update) | async-done | bytes 4718608 | tf_op jit(solution)/shard_map/all_gather | solution.py:110
  182.7 9.7 %collective-permute-done = bf16[128,1536]{1,0:T(8,128)(2,1)S(1)} collective-permute-done((bf16[128,1536]{1,0:T(8,128)(2,1)S(1)}, bf16[128,1536]{1,0:T(8,128)(2,1)S(1)}, u32[]{:S(2)}, u32[]{:S(2)}) %collective-permute-start) | collective-permute-done | bytes 393248 | tf_op jit(solution)/shard_map/ppermute | solution.py:64
  195.1 9.0 %collective-permute-done.3 = bf16[128,1536]{1,0:T(8,128)(2,1)S(1)} collective-permute-done((bf16[128,1536]{1,0:T(8,128)(2,1)S(1)}, bf16[128,1536]{1,0:T(8,128)(2,1)S(1)}, u32[]{:S(2)}, u32[]{:S(2)}) %collective-permute-start.3) | collective-permute-done | bytes 393248 | tf_op jit(solution)/shard_map/ppermute | solution.py:64
  224.6 4.7 all-to-all-start
  233.5 91.3 %all-to-all-done = bf16[4,2,384,560]{2,3,1,0:T(8,128)(2,1)} async-done(((bf16[4,2,384,560]{2,3,1,0:T(8,128)(2,1)}), bf16[4,2,384,560]{2,3,1,0:T(8,128)(2,1)}, u32[]{:S(2)}, u32[]{:S(2)}) %all-to-all-start) | async-done | bytes 3440672 | tf_op jit(solution)/shard_map/all_to_all | solution.py:134
  331.4 9.2 %fusion.73 = f32[2048,560]{0,1:T(8,128)} fusion(bf16[2048,1536]{1,0:T(8,128)(2,1)} %bitcast.252, bf16[1536,560]{0,1:T(8,128)(2,1)} %bitcast.274), kind=kOutput, calls=%fused_computation.187 | convolution fusion | flops 3523215360 | bytes 12599296 | tf_op jit(solution)/shard_map/dot_general | solution.py:60
  340.6 5.8 fusion.72
  346.4 10.8 %multiply_convert_fusion.1 = (bf16[2048,560]{0,1:T(8,128)(2,1)S(1)}, bf16[2048,560]{0,1:T(8,128)(2,1)S(1)}, bf16[2048,560]{0,1:T(8,128)(2,1)}) fusion(f32[2048,560]{0,1:T(8,128)} %fusion.72, f32[2048,560]{0,1:T(8,128)} %fusion.73, bf16[2048,1536]{1,0:T(8,128)(2,1)} %bitcast.290, bf16[280,1536]{1,0:T(8,128)(2,1)} %collective-permute-done.1, ...), kind=kOutput, calls=%fused_computation.6 | convolution fusion | flops 3545006080 | bytes 24068096 | tf_op jit(solution)/shard_map/dot_general | solution.py:60
  357.2 5.1 fusion.74
  362.4 7.0 add_convert_fusion
  371.0 8.9 %copy.168 = bf16[1536,2048]{1,0:T(8,128)(2,1)} copy(bf16[1536,2048]{0,1:T(8,128)(2,1)} %bitcast.253) | data formatting | bytes 12582912 | tf_op jit(solution)/shard_map/dot_general | solution.py:60
  379.9 50.9 %reduce-scatter.6.cloned.1.call-done = bf16[2,128,1536]{2,1,0:T(8,128)(2,1)} async-done(((bf16[2,1024,1536]{2,1,0:T(8,128)(2,1)}), bf16[2,128,1536]{2,1,0:T(8,128)(2,1)}) %reduce-scatter.6.cloned.1.call-update) | async-done | bytes 786448 | tf_op jit(solution)/shard_map/reduce_scatter | solution.py:73
  433.4 8.5 %fusion.10 = bf16[4,1,384,560]{2,3,0,1:T(8,128)(2,1)} fusion(bf16[4,384,2048]{2,1,0:T(8,128)(2,1)} %bitcast.256, bf16[2048,560]{0,1:T(8,128)(2,1)} %copy-done.46), kind=kOutput, calls=%fused_computation.28 | convolution fusion | flops 3523215360 | bytes 10305536 | tf_op jit(solution)/shard_map/dot_general | solution.py:60
  443.3 4.7 convolution_convert_fusion
  461.3 7.5 fusion.13
  471.3 4.9 all-to-all-start.5
  476.3 9.2 %fusion.24 = bf16[2048,1536]{1,0:T(8,128)(2,1)} fusion(bf16[2048,560]{0,1:T(8,128)(2,1)} %get-tuple-element.25, bf16[280,1536]{1,0:T(8,128)(2,1)} %collective-permute-done.1, bf16[280,1536]{1,0:T(8,128)(2,1)S(1)} %copy-done.31), kind=kOutput, calls=%fused_computation.46 | convolution fusion | flops 3526656000 | bytes 10305536 | tf_op jit(solution)/shard_map/dot_general | solution.py:60
  485.5 7.7 %fusion.77 = bf16[560,1536]{1,0:T(8,128)(2,1)S(1)} fusion(bf16[2048,560]{0,1:T(8,128)(2,1)} %get-tuple-element.25, bf16[2048,1536]{1,0:T(8,128)(2,1)} %bitcast.291), kind=kOutput, calls=%fused_computation.191 | convolution fusion | flops 3523215360 | bytes 10305536 | tf_op jit(solution)/shard_map/dot_general | solution.py:60
  496.1 93.0 %collective-permute-done.5 = bf16[280,1536]{1,0:T(8,128)(2,1)S(1)} collective-permute-done((bf16[280,1536]{1,0:T(8,128)(2,1)S(1)}, bf16[280,1536]{1,0:T(8,128)(2,1)S(1)}, u32[]{:S(2)}, u32[]{:S(2)}) %collective-permute-start.5) | collective-permute-done | bytes 860192 | tf_op jit(solution)/shard_map/ppermute | solution.py:229
  601.0 14.5 %all-to-all-done.7 = bf16[8,280,192]{2,1,0:T(8,128)(2,1)S(1)} async-done(((bf16[8,280,192]{2,1,0:T(8,128)(2,1)}), bf16[8,280,192]{2,1,0:T(8,128)(2,1)S(1)}, u32[]{:S(2)}, u32[]{:S(2)}) %all-to-all-start.7) | async-done | bytes 860192 | tf_op jit(solution)/shard_map/all_to_all | solution.py:231
  615.5 4.3 all-to-all-start.6
  619.8 4.7 copy.190
  629.0 13.4 %all-to-all-done.6 = bf16[8,1,384,280]{2,3,1,0:T(8,128)(2,1)} async-done(((bf16[8,1,384,280]{2,3,1,0:T(8,128)(2,1)}), bf16[8,1,384,280]{2,3,1,0:T(8,128)(2,1)}, u32[]{:S(2)}, u32[]{:S(2)}) %all-to-all-start.6) | async-done | bytes 1720352 | tf_op jit(solution)/shard_map/all_to_all | solution.py:217
  664.6 4.9 all-to-all-start.4
  674.3 9.8 %all-to-all-done.4 = bf16[4,384,192]{1,2,0:T(8,128)(2,1)S(1)} async-done(((bf16[4,384,192]{1,2,0:T(8,128)(2,1)}), bf16[4,384,192]{1,2,0:T(8,128)(2,1)S(1)}, u32[]{:S(2)}, u32[]{:S(2)}) %all-to-all-start.4) | async-done | bytes 589856 | tf_op jit(solution)/shard_map/all_to_all | solution.py:282
  690.3 7.0 all-to-all-done.1
  705.3 6.0 fusion.31
  711.6 39.9 %all-reduce = f32[32,160]{1,0:T(8,128)S(1)} all-reduce(f32[32,160]{1,0:T(8,128)S(1)} %pad_maximum_fusion.13), channel_id=6, replica_groups=mesh['ctx'=8,'fsdp'=4] {'ctx','fsdp'}, use_global_device_ids=true, to_apply=%region_15.16.clone | all-reduce | flops 5120 | bytes 40960
  (267 shorter events, 149.2 us)
Async XLA Ops:
  7.2 76.1 %all-gather.10.cloned.1.call-start = ((), (), s32[]{:S(2)}) async-start(), calls=%async_computation.11 | async-start | bytes 6488064 | tf_op jit(solution)/shard_map/all_gather | solution.py:104
  9.3 101.2 %all-gather.12.cloned.1.call-start = ((), (), s32[]{:S(2)}) async-start(), calls=%async_computation.12 | async-start | bytes 1179648 | tf_op jit(solution)/shard_map/all_gather | solution.py:159
  25.0 58.3 %copy-start.34 = (f32[1536]{0:T(1024)}, f32[1536]{0:T(1024)S(1)}, u32[]{:S(2)}) copy-start(f32[1536]{0:T(1024)S(1)} %reshape.492) | copy-start | bytes 18436
  26.1 65.0 %copy-start.23 = (f32[128,128]{0,1:T(8,128)}, f32[128,128]{0,1:T(8,128)S(1)}, u32[]{:S(2)}) copy-start(f32[128,128]{0,1:T(8,128)S(1)} %get-tuple-element.54) | copy-start | bytes 196612
  26.1 64.9 %copy-start.25 = (f32[128,128]{0,1:T(8,128)}, f32[128,128]{0,1:T(8,128)S(1)}, u32[]{:S(2)}) copy-start(f32[128,128]{0,1:T(8,128)S(1)} %get-tuple-element.55) | copy-start | bytes 196612
  26.2 61.3 %copy-start.32 = (f32[128,128]{1,0:T(8,128)}, f32[128,128]{1,0:T(8,128)S(1)}, u32[]{:S(2)}) copy-start(f32[128,128]{1,0:T(8,128)S(1)} %copy.142) | copy-start | bytes 196612
  28.6 58.5 %copy-start.6 = (bf16[128,1536]{1,0:T(8,128)(2,1)}, bf16[128,1536]{1,0:T(8,128)(2,1)S(1)}, u32[]{:S(2)}) copy-start(bf16[128,1536]{1,0:T(8,128)(2,1)S(1)} %fusion.25) | copy-start | bytes 1179652
  88.5 89.2 %all-gather.14.cloned.1.call-start = ((), (), s32[]{:S(2)}) async-start(), calls=%async_computation.13 | async-start | bytes 4866048 | tf_op jit(solution)/shard_map/all_gather | solution.py:110
  90.1 241.3 %all-gather.16.cloned.1.call-start = ((), (), s32[]{:S(2)}) async-start(), calls=%async_computation.14 | async-start | bytes 7077888 | tf_op jit(solution)/shard_map/all_gather | solution.py:69
  120.9 56.8 %copy-start.4 = (bf16[1,128,1536]{2,1,0:T(8,128)(2,1)S(1)}, bf16[1,128,1536]{2,1,0:T(8,128)(2,1)}, u32[]{:S(2)}) copy-start(bf16[1,128,1536]{2,1,0:T(8,128)(2,1)} %param.11) | copy-start | bytes 1179652
  123.7 57.2 %copy-start.7 = (bf16[2,6,128,128]{2,3,1,0:T(8,128)(2,1)}, bf16[2,6,128,128]{2,3,1,0:T(8,128)(2,1)S(1)}, u32[]{:S(2)}) copy-start(bf16[2,6,128,128]{2,3,1,0:T(8,128)(2,1)S(1)} %get-tuple-element.60) | copy-start | bytes 1179652
  181.1 11.3 %collective-permute-start = (bf16[128,1536]{1,0:T(8,128)(2,1)S(1)}, bf16[128,1536]{1,0:T(8,128)(2,1)S(1)}, u32[]{:S(2)}, u32[]{:S(2)}) collective-permute-start(bf16[128,1536]{1,0:T(8,128)(2,1)S(1)} %multiply_convert_fusion.4), channel_id=1, source_target_pairs={{0,1},{1,0},{2,3},{3,2},{4,5},{5,4},{6,7},{7,6},{8,9},{9,8},{10,11... | collective-permute-start | bytes 1179656 | tf_op jit(solution)/shard_map/ppermute | solution.py:64
  193.4 153.0 %all-gather.18.cloned.1.call-start = ((), (), s32[]{:S(2)}) async-start(), calls=%async_computation.16 | async-start | bytes 7077888 | tf_op jit(solution)/shard_map/all_gather | solution.py:69
  193.7 10.5 %collective-permute-start.3 = (bf16[128,1536]{1,0:T(8,128)(2,1)S(1)}, bf16[128,1536]{1,0:T(8,128)(2,1)S(1)}, u32[]{:S(2)}, u32[]{:S(2)}) collective-permute-start(bf16[128,1536]{1,0:T(8,128)(2,1)S(1)} %bitcast.262), channel_id=1, source_target_pairs={{0,1},{1,0},{2,3},{3,2},{4,5},{5,4},{6,7},{7,6},{8,9},{9,8},{10,11... | collective-permute-start | bytes 1179656 | tf_op jit(solution)/shard_map/ppermute | solution.py:64
  224.6 100.2 %all-to-all-start = ((bf16[4,2,384,560]{2,3,1,0:T(8,128)(2,1)}), bf16[4,2,384,560]{2,3,1,0:T(8,128)(2,1)}, u32[]{:S(2)}, u32[]{:S(2)}) async-start(bf16[4,2,384,560]{2,3,1,0:T(8,128)(2,1)} %pad_maximum_fusion), calls=%async_computation | async-start | bytes 6881280 | tf_op jit(solution)/shard_map/all_to_all | solution.py:134
  229.3 201.5 %reduce-scatter.6.cloned.1.call-start = ((), (), s32[]{:S(2)}) async-start(), calls=%async_computation.17 | async-start | bytes 7077888 | tf_op jit(solution)/shard_map/reduce_scatter | solution.py:73
  230.6 115.8 %copy-start.30 = (bf16[280,1536]{1,0:T(8,128)(2,1)}, bf16[280,1536]{1,0:T(8,128)(2,1)S(1)}, u32[]{:S(2)}) copy-start(bf16[280,1536]{1,0:T(8,128)(2,1)S(1)} %constant_dynamic-slice_fusion.10) | copy-start | bytes 2580484
  230.6 115.8 %collective-permute-start.1 = (bf16[280,1536]{1,0:T(8,128)(2,1)S(1)}, bf16[280,1536]{1,0:T(8,128)(2,1)}, u32[]{:S(2)}, u32[]{:S(2)}) collective-permute-start(bf16[280,1536]{1,0:T(8,128)(2,1)S(1)} %constant_dynamic-slice_fusion.10), channel_id=1, source_target_pairs={{2,0},{3,1},{0,2},{1,3},{6,4},{7,5},{4,6},{5,7},{10,8},{11,9},{8,1... | collective-permute-start | bytes 2580488 | tf_op jit(solution)/shard_map/ppermute | solution.py:141
  369.4 250.4 %all-gather.20.cloned.1.call-start = ((), (), s32[]{:S(2)}) async-start(), calls=%async_computation.19 | async-start | bytes 3538944 | tf_op jit(solution)/shard_map/all_gather | solution.py:272
  370.2 290.5 %all-gather.22.cloned.1.call-start = ((), (), s32[]{:S(2)}) async-start(), calls=%async_computation.20 | async-start | bytes 3538944 | tf_op jit(solution)/shard_map/all_gather | solution.py:272
  370.9 298.6 %reduce-scatter.8.cloned.1.call-start = ((), (), s32[]{:S(2)}) async-start(), calls=%async_computation.18 | async-start | bytes 1179648 | tf_op jit(solution)/shard_map/reduce_scatter | solution.py:255
  431.8 10.8 %collective-permute-start.4 = (bf16[128,1536]{1,0:T(8,128)(2,1)S(1)}, bf16[128,1536]{1,0:T(8,128)(2,1)S(1)}, u32[]{:S(2)}, u32[]{:S(2)}) collective-permute-start(bf16[128,1536]{1,0:T(8,128)(2,1)S(1)} %slice_bitcast_fusion), channel_id=1, source_target_pairs={{0,1},{1,0},{2,3},{3,2},{4,5},{5,4},{6,7},{7,6},{8,9},{9,8},{10,11... | collective-permute-start | bytes 1179656 | tf_op jit(solution)/shard_map/ppermute | solution.py:64
  471.3 122.2 %all-to-all-start.5 = ((bf16[4,2,384,560]{2,3,1,0:T(8,128)(2,1)}), bf16[4,2,384,560]{2,3,1,0:T(8,128)(2,1)}, u32[]{:S(2)}, u32[]{:S(2)}) async-start(bf16[4,2,384,560]{2,3,1,0:T(8,128)(2,1)} %copy.169), calls=%async_computation.8 | async-start | bytes 6881280 | tf_op jit(solution)/shard_map/all_to_all | solution.py:202
  476.2 211.4 %reduce-scatter.4.cloned.1.call-start = ((), (), s32[]{:S(2)}) async-start(), calls=%async_computation.15 | async-start | bytes 7077888 | tf_op jit(solution)/shard_map/reduce_scatter | solution.py:73
  493.3 95.9 %collective-permute-start.5 = (bf16[280,1536]{1,0:T(8,128)(2,1)S(1)}, bf16[280,1536]{1,0:T(8,128)(2,1)S(1)}, u32[]{:S(2)}, u32[]{:S(2)}) collective-permute-start(bf16[280,1536]{1,0:T(8,128)(2,1)S(1)} %slice.196), channel_id=1, source_target_pairs={{0,2},{1,3},{2,0},{3,1},{4,6},{5,7},{6,4},{7,5},{8,10},{9,11},{10,... | collective-permute-start | bytes 2580488 | tf_op jit(solution)/shard_map/ppermute | solution.py:229
  593.5 21.9 %all-to-all-start.7 = ((bf16[8,280,192]{2,1,0:T(8,128)(2,1)}), bf16[8,280,192]{2,1,0:T(8,128)(2,1)S(1)}, u32[]{:S(2)}, u32[]{:S(2)}) async-start(bf16[8,280,192]{2,1,0:T(8,128)(2,1)} %bitcast.245), calls=%async_computation.10 | async-start | bytes 2293760 | tf_op jit(solution)/shard_map/all_to_all | solution.py:231
  615.5 26.9 %all-to-all-start.6 = ((bf16[8,1,384,280]{2,3,1,0:T(8,128)(2,1)}), bf16[8,1,384,280]{2,3,1,0:T(8,128)(2,1)}, u32[]{:S(2)}, u32[]{:S(2)}) async-start(bf16[8,1,384,280]{2,3,1,0:T(8,128)(2,1)} %bitcast.249), calls=%async_computation.9 | async-start | bytes 3440640 | tf_op jit(solution)/shard_map/all_to_all | solution.py:217
  646.7 12.4 %all-to-all-start.3 = ((bf16[8,128,192]{1,2,0:T(8,128)(2,1)}), bf16[8,128,192]{1,2,0:T(8,128)(2,1)}, u32[]{:S(2)}, u32[]{:S(2)}) async-start(bf16[8,128,192]{1,2,0:T(8,128)(2,1)} %bitcast.68), calls=%async_computation.6 | async-start | bytes 786432 | tf_op jit(solution)/shard_map/all_to_all | solution.py:274
  664.6 19.6 %all-to-all-start.4 = ((bf16[4,384,192]{1,2,0:T(8,128)(2,1)}), bf16[4,384,192]{1,2,0:T(8,128)(2,1)S(1)}, u32[]{:S(2)}, u32[]{:S(2)}) async-start(bf16[4,384,192]{1,2,0:T(8,128)(2,1)} %fusion.76), calls=%async_computation.7 | async-start | bytes 1179648 | tf_op jit(solution)/shard_map/all_to_all | solution.py:282
  684.1 13.1 %all-to-all-start.1 = ((bf16[8,128,256]{2,1,0:T(8,128)(2,1)}), bf16[8,128,256]{2,1,0:T(8,128)(2,1)S(1)}, u32[]{:S(2)}, u32[]{:S(2)}) async-start(bf16[8,128,256]{2,1,0:T(8,128)(2,1)} %bitcast.60), calls=%async_computation.4 | async-start | bytes 1048576 | tf_op jit(solution)/shard_map/all_to_all | solution.py:274
  689.4 63.2 %collective-permute-start.2 = (bf16[128,1536]{1,0:T(8,128)(2,1)}, bf16[128,1536]{1,0:T(8,128)(2,1)}, u32[]{:S(2)}, u32[]{:S(2)}) collective-permute-start(bf16[128,1536]{1,0:T(8,128)(2,1)} %slice_bitcast_fusion.2), channel_id=1, source_target_pairs={{0,1},{1,0},{2,3},{3,2},{4,5},{5,4},{6,7},{7,6},{8,9},{9,8},{10,11... | collective-permute-start | bytes 1179656 | tf_op jit(solution)/shard_map/ppermute | solution.py:64
  701.0 54.7 %all-to-all-start.2 = ((bf16[4,384,256]{2,1,0:T(8,128)(2,1)}), bf16[4,384,256]{2,1,0:T(8,128)(2,1)}, u32[]{:S(2)}, u32[]{:S(2)}) async-start(bf16[4,384,256]{2,1,0:T(8,128)(2,1)} %fusion.75), calls=%async_computation.5 | async-start | bytes 1572864 | tf_op jit(solution)/shard_map/all_to_all | solution.py:282
  (40 other events, 463.1 us)
Sparse Core Ops, SparseCore 0:
  11.4 71.8 all-gather.9
  88.6 21.8 all-gather.11
  114.0 63.6 all-gather.13
  193.5 43.6 all-gather.15
  239.0 45.3 all-gather.17
  369.5 61.2 reduce-scatter.5
  432.7 32.1 all-gather.19
  466.8 32.7 all-gather.21
  502.7 35.9 reduce-scatter.7
  541.9 63.7 reduce-scatter.3
where the time goes:
time: 774 us; the launch traced here: 765 us
  waiting for transfers between devices  432 us (56%)
  matrix products  113 us (15%)
  local copies, waits for them, and re-layouts  66.2 us (9%)
  blocking collectives  54.8 us (7%)
  starting transfers between devices  45.1 us (6%)
  other arithmetic  37.7 us (5%)
  between operations  15.7 us (2%)
    dot_general x15, matrix products, dot(): lax.dot_general(left, right, (dims, ((), ())), preferred_element_type=out)  96.1 us
    ppermute x1, waiting for transfers between devices, body(): lax.ppermute(grad_down[b], 'fsdp', route).astype(F32)  93 us
    all_to_all x1, waiting for transfers between devices, body(): got = lax.all_to_all(sent, 'fsdp', split_axis=0, concat_axis=0, tiled=True)  91.3 us
    all_gather x1, waiting for transfers between devices, body(): lax.all_gather(lax.dynamic_slice_in_dim(projection, place * slab, slab, 0...  54.7 us
    all_gather x1, waiting for transfers between devices, body(): lax.all_gather(lax.dynamic_slice_in_dim(output_weight, place * slab, slab...  53.9 us
    reduce_scatter x2, waiting for transfers between devices, scatter_tokens(): parts = lax.psum_scatter(partial, 'ctx', scatter_dimension=1, tiled=True)  50.9 us
    unnamed x1, blocking collectives  39.9 us
    ppermute x4, waiting for transfers between devices, swapped(): return lax.ppermute(x, 'fsdp', [(i, i ^ 1) for i in range(size)])  19.5 us
  transfers between devices with their start and end apart: 24, of which 14 were waited for; matrix products, arithmetic and copies ran while one was open for 23% of the time, Pallas kernels for 0%

commit v1 on v0

--- a/solution.py
+++ b/solution.py
@@ -3,6 +3,7 @@
 import jax.numpy as jnp
 from jax import lax
 from jax.sharding import PartitionSpec as P
+from jax.lax import axis_index, axis_size, ppermute
 
 HEADS = 12
 KV_HEADS = 2
@@ -14,6 +15,23 @@
 NEGATIVE = -1e30
 BF = jnp.bfloat16
 F32 = jnp.float32
+
+
+def build_members_all_now(mine_x):
+    nodes = axis_size("ctx")
+    lanes = [(nth, (nth + 1) % nodes) for nth in range(nodes)]
+    frames = [(nth, (nth - 1) % nodes) for nth in range(nodes)]
+    high, v_next = ([mine_x], [mine_x])
+    for _ in range(nodes // 2):
+        z = ppermute(high[-1], axis_name="ctx", perm=lanes)
+        high.append(z)
+    for _ in range((nodes - 1) // 2):
+        vec_out = ppermute(v_next[-1], axis_name="ctx", perm=frames)
+        v_next.append(vec_out)
+    w_next = jnp.concatenate([*high[::-1], *v_next[1:]], axis=0)
+    fresh = axis_index("ctx")
+    w1 = jnp.roll(w_next, (fresh - nodes // 2) * mine_x.shape[0], axis=0)
+    return w1
 
 
 def rope_tables(places):
@@ -156,9 +174,7 @@
         sine,
     ).astype(BF)
     values = projected[:, query_width + key_width :].astype(BF)
-    pairs = lax.all_gather(
-        jnp.concatenate([keys.reshape(rows, key_width), values], axis=1), "ctx", axis=0, tiled=True
-    )
+    pairs = build_members_all_now(jnp.concatenate([keys.reshape(rows, key_width), values], axis=1))
     all_keys = pairs[:, :key_width].reshape(length, KV_HEADS, HEAD)
     all_values = pairs[:, key_width:].reshape(length, KV_HEADS, HEAD)
     grouped = queries.reshape(rows, KV_HEADS, ratio, HEAD).transpose(1, 2, 0, 3)

time: 774 us -> 742 us (0.959)
  waiting for transfers between devices: 432 us -> 394 us
  starting transfers between devices: 45.1 us -> 53.2 us
    all_gather x1, waiting for transfers between devices: 53.9 us -> 19.4 us  [body(): lax.all_gather(lax.dynamic_slice_in_dim(output_weight, place * slab, slab...]
    all_gather x1 -> x0, waiting for transfers between devices: 19.4 us -> none  [body(): lax.all_gather(jnp.concatenate([keys.reshape(rows, key_width), values], a...]
    ppermute x0 -> x7, waiting for transfers between devices: none -> 15.4 us  [the longest x4 15 us: build_members_all_now(): z = ppermute(high[-1], axis_name='ctx', perm=lanes)]
    ppermute x0 -> x7, starting transfers between devices: none -> 8.28 us  [the longest x3 8.02 us: build_members_all_now(): vec_out = ppermute(v_next[-1], axis_name='ctx', perm=frames)]
    unnamed x109 -> x106, local copies, waits for them, and re-layouts: 18.2 us -> 18.4 us
  transfers between devices with their start and end apart: 24 -> 30, of which waited for: 14 -> 18; matrix products, arithmetic and copies ran while one was open for 23% -> 25% of each run, Pallas kernels for 0% -> 0%
where the time goes in v1:
time: 742 us; the launch traced here: 733 us
  waiting for transfers between devices  394 us (53%)
  matrix products  110 us (15%)
  local copies, waits for them, and re-layouts  64.3 us (9%)
  blocking collectives  54.8 us (7%)
  starting transfers between devices  53.2 us (7%)
  other arithmetic  40.6 us (5%)
  between operations  15.5 us (2%)
    ppermute x1, waiting for transfers between devices, body(): lax.ppermute(grad_down[b], 'fsdp', route).astype(F32)  93.6 us
    dot_general x15, matrix products, dot(): lax.dot_general(left, right, (dims, ((), ())), preferred_element_type=out)  93.4 us
    all_to_all x1, waiting for transfers between devices, body(): got = lax.all_to_all(sent, 'fsdp', split_axis=0, concat_axis=0, tiled=True)  91.2 us
    all_gather x1, waiting for transfers between devices, body(): lax.all_gather(lax.dynamic_slice_in_dim(projection, place * slab, slab, 0...  51.3 us
    reduce_scatter x2, waiting for transfers between devices, scatter_tokens(): parts = lax.psum_scatter(partial, 'ctx', scatter_dimension=1, tiled=True)  51.1 us
    unnamed x1, blocking collectives  39.9 us
    all_gather x1, waiting for transfers between devices, body(): lax.all_gather(lax.dynamic_slice_in_dim(output_weight, place * slab, slab...  19.4 us
    ppermute x4, waiting for transfers between devices, swapped(): return lax.ppermute(x, 'fsdp', [(i, i ^ 1) for i in range(size)])  19.4 us
  transfers between devices with their start and end apart: 30, of which 18 were waited for; matrix products, arithmetic and copies ran while one was open for 25% of the time, Pallas kernels for 0%

profile of v1, /device:TPU:0, one launch (start us, length us, event | category | flops | bytes accessed | tf_op | source)
XLA Modules:
  0.0 733.0 jit_solution(14396253699496193858)
XLA Ops:
  11.8 15.0 %all-gather.1 = bf16[4,1,1280]{2,1,0:T(2,128)(2,1)S(1)} all-gather(bf16[1,1,1280]{2,1,0:T(2,128)(2,1)S(1)} %reshape.500), channel_id=2, replica_groups=mesh['ctx'=8,'fsdp'=4] {'fsdp'}, dimensions={0}, use_global_device_ids=true | all-gather | bytes 12800 | tf_op jit(solution)/shard_map/all_gather | solution.py:134
  31.9 51.3 %all-gather.9.cloned.1.call-done = bf16[1536,2048]{1,0:T(8,128)(2,1)} async-done(((bf16[48,2048]{1,0:T(8,128)(2,1)}), bf16[1536,2048]{1,0:T(8,128)(2,1)}) %all-gather.9.cloned.1.call-update) | async-done | bytes 6291472 | tf_op jit(solution)/shard_map/all_gather | solution.py:122
  88.7 5.2 collective-permute-done
  118.2 4.8 fusion.70
  130.3 19.4 %all-gather.11.cloned.1.call-done = bf16[1536,1536]{1,0:T(8,128)(2,1)} async-done(((bf16[48,1536]{1,0:T(8,128)(2,1)}), bf16[1536,1536]{1,0:T(8,128)(2,1)}) %all-gather.11.cloned.1.call-update) | async-done | bytes 4718608 | tf_op jit(solution)/shard_map/all_gather | solution.py:128
  154.8 9.7 %collective-permute-done.7 = bf16[128,1536]{1,0:T(8,128)(2,1)S(1)} collective-permute-done((bf16[128,1536]{1,0:T(8,128)(2,1)S(1)}, bf16[128,1536]{1,0:T(8,128)(2,1)S(1)}, u32[]{:S(2)}, u32[]{:S(2)}) %collective-permute-start.7) | collective-permute-done | bytes 393248 | tf_op jit(solution)/shard_map/ppermute | solution.py:82
  167.2 9.0 %collective-permute-done.10 = bf16[128,1536]{1,0:T(8,128)(2,1)S(1)} collective-permute-done((bf16[128,1536]{1,0:T(8,128)(2,1)S(1)}, bf16[128,1536]{1,0:T(8,128)(2,1)S(1)}, u32[]{:S(2)}, u32[]{:S(2)}) %collective-permute-start.10) | collective-permute-done | bytes 393248 | tf_op jit(solution)/shard_map/ppermute | solution.py:82
  192.8 4.7 all-to-all-start
  201.7 91.2 %all-to-all-done = bf16[4,2,384,560]{2,3,1,0:T(8,128)(2,1)} async-done(((bf16[4,2,384,560]{2,3,1,0:T(8,128)(2,1)}), bf16[4,2,384,560]{2,3,1,0:T(8,128)(2,1)}, u32[]{:S(2)}, u32[]{:S(2)}) %all-to-all-start) | async-done | bytes 3440672 | tf_op jit(solution)/shard_map/all_to_all | solution.py:152
  299.5 9.2 %fusion.73 = f32[2048,560]{0,1:T(8,128)} fusion(bf16[2048,1536]{1,0:T(8,128)(2,1)} %bitcast.254, bf16[1536,560]{0,1:T(8,128)(2,1)} %bitcast.276), kind=kOutput, calls=%fused_computation.204 | convolution fusion | flops 3523215360 | bytes 12599296 | tf_op jit(solution)/shard_map/dot_general | solution.py:78
  308.7 5.8 fusion.72
  314.5 10.8 %multiply_convert_fusion.1 = (bf16[2048,560]{0,1:T(8,128)(2,1)S(1)}, bf16[2048,560]{0,1:T(8,128)(2,1)S(1)}, bf16[2048,560]{0,1:T(8,128)(2,1)}) fusion(f32[2048,560]{0,1:T(8,128)} %fusion.72, f32[2048,560]{0,1:T(8,128)} %fusion.73, bf16[2048,1536]{1,0:T(8,128)(2,1)} %bitcast.292, bf16[280,1536]{1,0:T(8,128)(2,1)} %collective-permute-done.8, ...), kind=kOutput, calls=%fused_computation.6 | convolution fusion | flops 3545006080 | bytes 24068096 | tf_op jit(solution)/shard_map/dot_general | solution.py:78
  325.3 5.1 fusion.74
  330.4 7.0 add_convert_fusion
  338.9 9.1 %copy.168 = bf16[1536,2048]{1,0:T(8,128)(2,1)} copy(bf16[1536,2048]{0,1:T(8,128)(2,1)} %bitcast.255) | data formatting | bytes 12582912 | tf_op jit(solution)/shard_map/dot_general | solution.py:78
  348.0 51.1 %reduce-scatter.6.cloned.1.call-done = bf16[2,128,1536]{2,1,0:T(8,128)(2,1)} async-done(((bf16[2,1024,1536]{2,1,0:T(8,128)(2,1)}), bf16[2,128,1536]{2,1,0:T(8,128)(2,1)}) %reduce-scatter.6.cloned.1.call-update) | async-done | bytes 786448 | tf_op jit(solution)/shard_map/reduce_scatter | solution.py:91
  401.7 8.6 %fusion.10 = bf16[4,1,384,560]{2,3,0,1:T(8,128)(2,1)} fusion(bf16[4,384,2048]{2,1,0:T(8,128)(2,1)} %bitcast.258, bf16[2048,560]{0,1:T(8,128)(2,1)} %copy-done.36), kind=kOutput, calls=%fused_computation.28 | convolution fusion | flops 3523215360 | bytes 10305536 | tf_op jit(solution)/shard_map/dot_general | solution.py:78
  426.5 7.4 %fusion.13 = bf16[4,1,384,560]{2,3,0,1:T(8,128)(2,1)S(1)} fusion(bf16[4,384,2048]{2,1,0:T(8,128)(2,1)} %bitcast.259, bf16[2048,560]{0,1:T(8,128)(2,1)} %copy-done.37), kind=kOutput, calls=%fused_computation.29 | convolution fusion | flops 3523215360 | bytes 10305536 | tf_op jit(solution)/shard_map/dot_general | solution.py:78
  436.5 4.8 all-to-all-start.5
  441.3 9.3 %fusion.24 = bf16[2048,1536]{1,0:T(8,128)(2,1)} fusion(bf16[2048,560]{0,1:T(8,128)(2,1)} %get-tuple-element.25, bf16[280,1536]{1,0:T(8,128)(2,1)} %collective-permute-done.8, bf16[280,1536]{1,0:T(8,128)(2,1)S(1)} %copy-done.28), kind=kOutput, calls=%fused_computation.46 | convolution fusion | flops 3526656000 | bytes 10305536 | tf_op jit(solution)/shard_map/dot_general | solution.py:78
  450.6 7.2 fusion.77
  460.8 93.6 %collective-permute-done.12 = bf16[280,1536]{1,0:T(8,128)(2,1)S(1)} collective-permute-done((bf16[280,1536]{1,0:T(8,128)(2,1)S(1)}, bf16[280,1536]{1,0:T(8,128)(2,1)S(1)}, u32[]{:S(2)}, u32[]{:S(2)}) %collective-permute-start.12) | collective-permute-done | bytes 860192 | tf_op jit(solution)/shard_map/ppermute | solution.py:245
  566.1 17.7 %all-to-all-done.7 = bf16[8,280,192]{2,1,0:T(8,128)(2,1)S(1)} async-done(((bf16[8,280,192]{2,1,0:T(8,128)(2,1)}), bf16[8,280,192]{2,1,0:T(8,128)(2,1)S(1)}, u32[]{:S(2)}, u32[]{:S(2)}) %all-to-all-start.7) | async-done | bytes 860192 | tf_op jit(solution)/shard_map/all_to_all | solution.py:247
  583.7 4.3 all-to-all-start.6
  588.1 4.7 copy.190
  597.3 13.4 %all-to-all-done.6 = bf16[8,1,384,280]{2,3,1,0:T(8,128)(2,1)} async-done(((bf16[8,1,384,280]{2,3,1,0:T(8,128)(2,1)}), bf16[8,1,384,280]{2,3,1,0:T(8,128)(2,1)}, u32[]{:S(2)}, u32[]{:S(2)}) %all-to-all-start.6) | async-done | bytes 1720352 | tf_op jit(solution)/shard_map/all_to_all | solution.py:233
  632.8 5.0 all-to-all-start.4
  642.6 9.8 %all-to-all-done.4 = bf16[4,384,192]{1,2,0:T(8,128)(2,1)S(1)} async-done(((bf16[4,384,192]{1,2,0:T(8,128)(2,1)}), bf16[4,384,192]{1,2,0:T(8,128)(2,1)S(1)}, u32[]{:S(2)}, u32[]{:S(2)}) %all-to-all-start.4) | async-done | bytes 589856 | tf_op jit(solution)/shard_map/all_to_all | solution.py:298
  658.6 7.0 all-to-all-done.1
  669.4 4.2 all-to-all-start.2
  673.6 6.0 fusion.31
  679.9 39.9 %all-reduce = f32[32,160]{1,0:T(8,128)S(1)} all-reduce(f32[32,160]{1,0:T(8,128)S(1)} %pad_maximum_fusion.13), channel_id=6, replica_groups=mesh['ctx'=8,'fsdp'=4] {'ctx','fsdp'}, use_global_device_ids=true, to_apply=%region_15.16.clone | all-reduce | flops 5120 | bytes 40960
  (279 shorter events, 166.2 us)
Async XLA Ops:
  7.2 76.1 %all-gather.9.cloned.1.call-start = ((), (), s32[]{:S(2)}) async-start(), calls=%async_computation.11 | async-start | bytes 6488064 | tf_op jit(solution)/shard_map/all_gather | solution.py:122
  9.3 140.5 %all-gather.11.cloned.1.call-start = ((), (), s32[]{:S(2)}) async-start(), calls=%async_computation.12 | async-start | bytes 4866048 | tf_op jit(solution)/shard_map/all_gather | solution.py:128
  11.0 288.5 %all-gather.13.cloned.1.call-start = ((), (), s32[]{:S(2)}) async-start(), calls=%async_computation.13 | async-start | bytes 7077888 | tf_op jit(solution)/shard_map/all_gather | solution.py:87
  27.8 79.7 %copy-start.23 = (f32[128,128]{0,1:T(8,128)}, f32[128,128]{0,1:T(8,128)S(1)}, u32[]{:S(2)}) copy-start(f32[128,128]{0,1:T(8,128)S(1)} %get-tuple-element.54) | copy-start | bytes 196612
  88.4 5.5 collective-permute-start
  93.9 7.3 collective-permute-start.1
  94.7 6.6 collective-permute-start.4
  101.2 6.3 collective-permute-start.2
  101.3 6.4 collective-permute-start.5
  107.5 5.6 collective-permute-start.3
  107.7 7.7 %collective-permute-start.6 = (bf16[128,512]{1,0:T(8,128)(2,1)S(1)}, bf16[128,512]{1,0:T(8,128)(2,1)S(1)}, u32[]{:S(2)}, u32[]{:S(2)}) collective-permute-start(bf16[128,512]{1,0:T(8,128)(2,1)S(1)} %collective-permute-done.5), channel_id=1, source_target_pairs={{0,28},{4,0},{8,4},{12,8},{16,12},{20,16},{24,20},{28,24},{1,29},{... | collective-permute-start | bytes 393224 | tf_op jit(solution)/shard_map/ppermute | solution.py:29
  153.2 11.3 %collective-permute-start.7 = (bf16[128,1536]{1,0:T(8,128)(2,1)S(1)}, bf16[128,1536]{1,0:T(8,128)(2,1)S(1)}, u32[]{:S(2)}, u32[]{:S(2)}) collective-permute-start(bf16[128,1536]{1,0:T(8,128)(2,1)S(1)} %multiply_convert_fusion.4), channel_id=1, source_target_pairs={{0,1},{1,0},{2,3},{3,2},{4,5},{5,4},{6,7},{7,6},{8,9},{9,8},{10,11... | collective-permute-start | bytes 1179656 | tf_op jit(solution)/shard_map/ppermute | solution.py:82
  165.5 149.0 %all-gather.15.cloned.1.call-start = ((), (), s32[]{:S(2)}) async-start(), calls=%async_computation.15 | async-start | bytes 7077888 | tf_op jit(solution)/shard_map/all_gather | solution.py:87
  165.7 10.5 %collective-permute-start.10 = (bf16[128,1536]{1,0:T(8,128)(2,1)S(1)}, bf16[128,1536]{1,0:T(8,128)(2,1)S(1)}, u32[]{:S(2)}, u32[]{:S(2)}) collective-permute-start(bf16[128,1536]{1,0:T(8,128)(2,1)S(1)} %bitcast.264), channel_id=1, source_target_pairs={{0,1},{1,0},{2,3},{3,2},{4,5},{5,4},{6,7},{7,6},{8,9},{9,8},{10,11... | collective-permute-start | bytes 1179656 | tf_op jit(solution)/shard_map/ppermute | solution.py:82
  192.8 100.0 %all-to-all-start = ((bf16[4,2,384,560]{2,3,1,0:T(8,128)(2,1)}), bf16[4,2,384,560]{2,3,1,0:T(8,128)(2,1)}, u32[]{:S(2)}, u32[]{:S(2)}) async-start(bf16[4,2,384,560]{2,3,1,0:T(8,128)(2,1)} %pad_maximum_fusion), calls=%async_computation | async-start | bytes 6881280 | tf_op jit(solution)/shard_map/all_to_all | solution.py:152
  197.5 201.5 %reduce-scatter.6.cloned.1.call-start = ((), (), s32[]{:S(2)}) async-start(), calls=%async_computation.16 | async-start | bytes 7077888 | tf_op jit(solution)/shard_map/reduce_scatter | solution.py:91
  198.8 115.6 %copy-start.27 = (bf16[280,1536]{1,0:T(8,128)(2,1)}, bf16[280,1536]{1,0:T(8,128)(2,1)S(1)}, u32[]{:S(2)}) copy-start(bf16[280,1536]{1,0:T(8,128)(2,1)S(1)} %constant_dynamic-slice_fusion.10) | copy-start | bytes 2580484
  198.8 115.6 %collective-permute-start.8 = (bf16[280,1536]{1,0:T(8,128)(2,1)S(1)}, bf16[280,1536]{1,0:T(8,128)(2,1)}, u32[]{:S(2)}, u32[]{:S(2)}) collective-permute-start(bf16[280,1536]{1,0:T(8,128)(2,1)S(1)} %constant_dynamic-slice_fusion.10), channel_id=1, source_target_pairs={{2,0},{3,1},{0,2},{1,3},{6,4},{7,5},{4,6},{5,7},{10,8},{11,9},{8,1... | collective-permute-start | bytes 2580488 | tf_op jit(solution)/shard_map/ppermute | solution.py:159
  337.5 250.6 %all-gather.17.cloned.1.call-start = ((), (), s32[]{:S(2)}) async-start(), calls=%async_computation.18 | async-start | bytes 3538944 | tf_op jit(solution)/shard_map/all_gather | solution.py:288
  338.1 290.8 %all-gather.19.cloned.1.call-start = ((), (), s32[]{:S(2)}) async-start(), calls=%async_computation.19 | async-start | bytes 3538944 | tf_op jit(solution)/shard_map/all_gather | solution.py:288
  338.8 299.0 %reduce-scatter.8.cloned.1.call-start = ((), (), s32[]{:S(2)}) async-start(), calls=%async_computation.17 | async-start | bytes 1179648 | tf_op jit(solution)/shard_map/reduce_scatter | solution.py:271
  400.1 10.8 %collective-permute-start.11 = (bf16[128,1536]{1,0:T(8,128)(2,1)S(1)}, bf16[128,1536]{1,0:T(8,128)(2,1)S(1)}, u32[]{:S(2)}, u32[]{:S(2)}) collective-permute-start(bf16[128,1536]{1,0:T(8,128)(2,1)S(1)} %slice_bitcast_fusion), channel_id=1, source_target_pairs={{0,1},{1,0},{2,3},{3,2},{4,5},{5,4},{6,7},{7,6},{8,9},{9,8},{10,11... | collective-permute-start | bytes 1179656 | tf_op jit(solution)/shard_map/ppermute | solution.py:82
  436.5 122.2 %all-to-all-start.5 = ((bf16[4,2,384,560]{2,3,1,0:T(8,128)(2,1)}), bf16[4,2,384,560]{2,3,1,0:T(8,128)(2,1)}, u32[]{:S(2)}, u32[]{:S(2)}) async-start(bf16[4,2,384,560]{2,3,1,0:T(8,128)(2,1)} %copy.169), calls=%async_computation.8 | async-start | bytes 6881280 | tf_op jit(solution)/shard_map/all_to_all | solution.py:218
  441.3 214.7 %reduce-scatter.4.cloned.1.call-start = ((), (), s32[]{:S(2)}) async-start(), calls=%async_computation.14 | async-start | bytes 7077888 | tf_op jit(solution)/shard_map/reduce_scatter | solution.py:91
  457.9 96.4 %collective-permute-start.12 = (bf16[280,1536]{1,0:T(8,128)(2,1)S(1)}, bf16[280,1536]{1,0:T(8,128)(2,1)S(1)}, u32[]{:S(2)}, u32[]{:S(2)}) collective-permute-start(bf16[280,1536]{1,0:T(8,128)(2,1)S(1)} %slice.194), channel_id=1, source_target_pairs={{0,2},{1,3},{2,0},{3,1},{4,6},{5,7},{6,4},{7,5},{8,10},{9,11},{10,... | collective-permute-start | bytes 2580488 | tf_op jit(solution)/shard_map/ppermute | solution.py:245
  558.7 25.1 %all-to-all-start.7 = ((bf16[8,280,192]{2,1,0:T(8,128)(2,1)}), bf16[8,280,192]{2,1,0:T(8,128)(2,1)S(1)}, u32[]{:S(2)}, u32[]{:S(2)}) async-start(bf16[8,280,192]{2,1,0:T(8,128)(2,1)} %bitcast.245), calls=%async_computation.10 | async-start | bytes 2293760 | tf_op jit(solution)/shard_map/all_to_all | solution.py:247
  583.7 26.9 %all-to-all-start.6 = ((bf16[8,1,384,280]{2,3,1,0:T(8,128)(2,1)}), bf16[8,1,384,280]{2,3,1,0:T(8,128)(2,1)}, u32[]{:S(2)}, u32[]{:S(2)}) async-start(bf16[8,1,384,280]{2,3,1,0:T(8,128)(2,1)} %bitcast.251), calls=%async_computation.9 | async-start | bytes 3440640 | tf_op jit(solution)/shard_map/all_to_all | solution.py:233
  615.0 12.4 %all-to-all-start.3 = ((bf16[8,128,192]{1,2,0:T(8,128)(2,1)}), bf16[8,128,192]{1,2,0:T(8,128)(2,1)}, u32[]{:S(2)}, u32[]{:S(2)}) async-start(bf16[8,128,192]{1,2,0:T(8,128)(2,1)} %bitcast.68), calls=%async_computation.6 | async-start | bytes 786432 | tf_op jit(solution)/shard_map/all_to_all | solution.py:290
  632.8 19.6 %all-to-all-start.4 = ((bf16[4,384,192]{1,2,0:T(8,128)(2,1)}), bf16[4,384,192]{1,2,0:T(8,128)(2,1)S(1)}, u32[]{:S(2)}, u32[]{:S(2)}) async-start(bf16[4,384,192]{1,2,0:T(8,128)(2,1)} %fusion.76), calls=%async_computation.7 | async-start | bytes 1179648 | tf_op jit(solution)/shard_map/all_to_all | solution.py:298
  652.4 13.1 %all-to-all-start.1 = ((bf16[8,128,256]{2,1,0:T(8,128)(2,1)}), bf16[8,128,256]{2,1,0:T(8,128)(2,1)S(1)}, u32[]{:S(2)}, u32[]{:S(2)}) async-start(bf16[8,128,256]{2,1,0:T(8,128)(2,1)} %bitcast.60), calls=%async_computation.4 | async-start | bytes 1048576 | tf_op jit(solution)/shard_map/all_to_all | solution.py:290
  657.7 63.2 %collective-permute-start.9 = (bf16[128,1536]{1,0:T(8,128)(2,1)}, bf16[128,1536]{1,0:T(8,128)(2,1)}, u32[]{:S(2)}, u32[]{:S(2)}) collective-permute-start(bf16[128,1536]{1,0:T(8,128)(2,1)} %slice_bitcast_fusion.2), channel_id=1, source_target_pairs={{0,1},{1,0},{2,3},{3,2},{4,5},{5,4},{6,7},{7,6},{8,9},{9,8},{10,11... | collective-permute-start | bytes 1179656 | tf_op jit(solution)/shard_map/ppermute | solution.py:82
  669.4 54.6 %all-to-all-start.2 = ((bf16[4,384,256]{2,1,0:T(8,128)(2,1)}), bf16[4,384,256]{2,1,0:T(8,128)(2,1)}, u32[]{:S(2)}, u32[]{:S(2)}) async-start(bf16[4,384,256]{2,1,0:T(8,128)(2,1)} %fusion.75), calls=%async_computation.5 | async-start | bytes 1572864 | tf_op jit(solution)/shard_map/all_to_all | solution.py:298
  (38 other events, 703.2 us)
Sparse Core Ops, SparseCore 0:
  11.4 71.7 all-gather.8
  86.7 62.9 all-gather.10
  165.6 43.6 all-gather.12
  211.1 45.3 all-gather.14
  337.6 61.4 reduce-scatter.5
  400.8 32.1 all-gather.16
  434.9 32.7 all-gather.18
  470.9 35.9 reduce-scatter.7
  510.3 69.9 reduce-scatter.3
